TPU v7x, 32 devices: a whole 2x2x4 slice. The times are simulated.
32 devices in a mesh: gx: 4 (over y, core), gy: 2 (over x), var: 4 (over z).
Axes of the slice: x: 2, y: 2, z: 4, core: 2. Of those that a mesh axis runs over, the one named last changes fastest.
Arguments:
- field: float32 [4, 32, 256, 256], P('var', None, 'gx', 'gy'), may hold values from -12 to 12
- drive: float32 [4, 32, 40, 40], P('var'), may hold values from -1 to 1
- keep_count: int32 [32], replicated, may hold values from 20 to 79, as said below
- level_class: int32 [32], replicated, may hold values from 0 to 7
- height_table: float32 [8], replicated, may hold values from 0.2 to 1
Outputs:
- nudged: float32 [4, 32, 256, 256], P('var', None, 'gx', 'gy')
Inputs may be any that keep to these rules, and one draw needn't show every extreme that they name: `keep_count`: some level in every draw has the count 2 * 40 - 1, which keeps all 40 x 40 modes.
All inputs are finite; a program needn't handle non-finite values.
Results may differ from a plain program's by a relative error of at most 0.0001.
Values sent between devices are 32-bit elements; how exact they have to be, the bound alone decides.
No kernel may reach another device: no remote copies, remote signals or barrier semaphores. Data moves between devices by JAX's collectives and lax.ppermute only.
A program may use at most 64 MiB of HBM per device.

v0:
```python
import functools

import numpy as np

import jax
import jax.numpy as jnp
from jax import lax
from jax.experimental import pallas as pl
from jax.experimental.pallas import tpu as pltpu
from jax.sharding import PartitionSpec as P


energy_weights = (1.0, 1.0, 2.0, 3.0)
strength_top = 0.5
epsilon = 1e-06


LANES = 128
VMEM = pltpu.MemorySpace.VMEM
SMEM = pltpu.MemorySpace.SMEM
HBM = pltpu.MemorySpace.HBM


def cosine_table(total, modes):
    cells = np.arange(total, dtype=np.int64)
    waves = np.arange(modes, dtype=np.int64)
    phase = waves[None, :] * (2 * cells[:, None] + 1) % (4 * total)
    factor = np.where(waves == 0, 1.0, np.sqrt(2.0))
    return (np.cos(np.pi * phase / (2.0 * total)) * factor[None, :]).astype(np.float32)


def dot(a, b):
    return jnp.dot(a, b, preferred_element_type=jnp.float32)


def split(x):
    high = x.astype(jnp.bfloat16)
    return high, (x - high.astype(jnp.float32)).astype(jnp.bfloat16)


def stack_split(x, axis):
    return jnp.concatenate(split(x), axis=axis)


def split_table(table, axis):
    high = table.astype(jnp.bfloat16)
    low = (table - high.astype(np.float32)).astype(jnp.bfloat16)
    top = np.concatenate([high, high], axis=axis)
    return np.concatenate([top, np.concatenate([low, np.zeros_like(low)], axis=axis)], axis=3 - axis)


def owned_half():
    at_x, at_y = lax.axis_index("gx"), lax.axis_index("gy")
    return lax.rem(at_x + at_x // 2 + at_y, 2)


def pack_lanes(pieces, modes):
    tiles = -(-len(pieces) * modes // LANES)
    out = [None] * tiles
    lane = lax.broadcasted_iota(jnp.int32, pieces[0].shape, 1)

    def put(tile, value):
        out[tile] = value if out[tile] is None else out[tile] + value

    for index, piece in enumerate(pieces):
        tile, offset = divmod(index * modes, LANES)
        turned = pltpu.roll(piece, offset, 1) if offset else piece
        if offset + modes > LANES:
            put(tile, jnp.where(lane >= offset, turned, 0.0))
            put(tile + 1, jnp.where(lane < offset, turned, 0.0))
        else:
            put(tile, turned)
    return out


def unpack_lanes(tiles, count, modes):
    lane = lax.broadcasted_iota(jnp.int32, tiles[0].shape, 1)
    pieces = []
    for index in range(count):
        tile, offset = divmod(index * modes, LANES)
        piece = tiles[tile]
        if offset + modes > LANES:
            piece = jnp.where(lane >= offset, piece, tiles[tile + 1])
        pieces.append(pltpu.roll(piece, LANES - offset, 1) if offset else piece)
    return pieces


def transform(block, tx, ty, modes):
    wide = stack_split(jnp.concatenate(block, axis=1), 0)
    both = dot(tx, wide)
    part = both[:modes] + both[modes:]
    tall = jnp.concatenate([part[:, l * LANES : (l + 1) * LANES] for l in range(len(block))], axis=0)
    both = dot(stack_split(tall, 1), ty)
    coeff = both[:, :LANES] + both[:, LANES:]
    return [coeff[l * modes : (l + 1) * modes] for l in range(len(block))]


def store_packed(out_ref, pieces, modes):
    for t, tile in enumerate(pack_lanes(pieces, modes)):
        out_ref[:, t * LANES : (t + 1) * LANES] = tile


def send_kernel(field_ref, tx_ref, ty_ref, block_ref, send_ref, tx, ty, sems):
    half = block_ref.shape[0] // 2
    modes = send_ref.shape[0]
    at_x, at_y = lax.axis_index("gx"), lax.axis_index("gy")
    core = owned_half()
    first = (1 - core) * half
    starts = [first, core * half]
    copies = [
        pltpu.make_async_copy(tx_ref.at[at_x], tx, sems.at[0]),
        pltpu.make_async_copy(ty_ref.at[at_y], ty, sems.at[1]),
    ]
    for q, (start, size) in enumerate(zip(starts, (half, half))):
        rows = pl.ds(start, size)
        copies.append(
            pltpu.make_async_copy(field_ref.at[0, rows], block_ref.at[rows], sems.at[2 + q])
        )
    for copy in copies:
        copy.start()
    copies[0].wait()
    copies[1].wait()
    pieces = []
    for q in range(1):
        copies[2 + q].wait()
        levels = [block_ref[first + l] for l in range(half)]
        pieces += transform(levels, tx[...], ty[...], modes)
    store_packed(send_ref, pieces, modes)
    copies[3].wait()


def keep_kernel(block_ref, tx_ref, ty_ref, keep_ref):
    half = block_ref.shape[0] // 2
    modes = keep_ref.shape[0]
    first = owned_half() * half
    levels = [block_ref[first + l] for l in range(half)]
    store_packed(keep_ref, transform(levels, tx_ref[...], ty_ref[...], modes), modes)


def prepare_kernel(
    _,
    keep_count_ref,
    class_ref,
    height_ref,
    drive_ref,
    tx_ref,
    ty_ref,
    goal_ref,
    mask_ref,
    lift_ref,
    tx_out_ref,
    ty_out_ref,
    drive,
    sems,
):
    half, modes, _ = drive.shape
    width = goal_ref.shape[1]
    at_x, at_y = lax.axis_index("gx"), lax.axis_index("gy")
    first = owned_half() * half
    copies = [
        pltpu.make_async_copy(drive_ref.at[0, pl.ds(first, half)], drive, sems.at[0]),
        pltpu.make_async_copy(tx_ref.at[at_x], tx_out_ref, sems.at[1]),
        pltpu.make_async_copy(ty_ref.at[at_y], ty_out_ref, sems.at[2]),
    ]
    for copy in copies:
        copy.start()
    for l in range(lift_ref.shape[0]):
        lift_ref[l : l + 1, :] = jnp.full((1, LANES), height_ref[class_ref[l]], jnp.float32)
    lane = lax.broadcasted_iota(jnp.int32, (8, LANES), 1)
    row = lax.broadcasted_iota(jnp.int32, (8, LANES), 0)
    for t in range(width // LANES):
        limit = jnp.zeros((8, LANES), jnp.int32)
        for l in range(t * LANES // modes, min(half, ((t + 1) * LANES - 1) // modes + 1)):
            wave = lane + (t * LANES - l * modes)
            limit = jnp.where(wave >= 0, keep_count_ref[first + l] - wave, limit)
        for r in range(0, modes, 8):
            mask_ref[r : r + 8, t * LANES : (t + 1) * LANES] = (row + r < limit).astype(jnp.float32)
    copies[0].wait()
    pad = jnp.zeros((modes, LANES - modes), jnp.float32)
    goal = pack_lanes([jnp.concatenate([drive[l], pad], axis=1) for l in range(half)], modes)
    for t, tile in enumerate(goal):
        goal_ref[:, t * LANES : (t + 1) * LANES] = tile
    for copy in copies[1:]:
        copy.wait()


def settle_kernel(goal_ref, mask_ref, own_ref, *rest):
    *others, delta_ref, energy_ref = rest
    modes, width = own_ref.shape
    variable = lax.axis_index("var")
    weight = jnp.float32(0.0)
    for index, value in enumerate(energy_weights):
        weight = jnp.where(variable == index, jnp.float32(value), weight)
    gap = jnp.zeros((8, LANES), jnp.float32)
    model = jnp.zeros((8, LANES), jnp.float32)
    for t in range(width // LANES):
        for r in range(0, modes, 8):
            at = (slice(r, r + 8), slice(t * LANES, (t + 1) * LANES))
            coeff = own_ref[at]
            for other in others:
                coeff = coeff + other[at]
            mask = mask_ref[at]
            delta = mask * (goal_ref[at] - coeff)
            delta_ref[at] = delta
            gap = gap + delta * delta
            model = model + mask * coeff * coeff
    gap = jnp.sum(gap, axis=0, keepdims=True)
    model = jnp.sum(model, axis=0, keepdims=True)
    energy_ref[...] = weight * jnp.where(lax.broadcasted_iota(jnp.int32, (8, LANES), 0) == 0, gap, model)


def inverse_kernel(which, delta_ref, lift_ref, tx_ref, ty_ref, out_ref):
    half, rows, _ = out_ref.shape
    modes, width = delta_ref.shape
    first = jnp.bitwise_xor(owned_half(), which) * half
    tiles = [delta_ref[:, t * LANES : (t + 1) * LANES] for t in range(width // LANES)]
    tall = jnp.concatenate(unpack_lanes(tiles, half, modes), axis=0)
    both = dot(stack_split(tall, 1), ty_ref[...])
    back = both[:, :LANES] + both[:, LANES:]
    wide = jnp.concatenate([back[l * modes : (l + 1) * modes] for l in range(half)], axis=1)
    both = dot(tx_ref[...], stack_split(wide, 0))
    for l in range(half):
        at = slice(l * LANES, (l + 1) * LANES)
        out_ref[l] = lift_ref[pl.ds(first + l, 1), :] * (both[:rows, at] + both[rows:, at])


def finish_kernel(energy_ref, last_ref, block_ref, own_ref, other_ref, out_ref, buffer, sems):
    half = own_ref.shape[0]
    core = owned_half()
    energy = energy_ref[...] + last_ref[...]
    gap = jnp.sum(energy[:1], keepdims=True)
    model = jnp.sum(energy[1:2], keepdims=True)
    strength = strength_top * gap / (gap + model + epsilon)
    count = sems.shape[0] // 2
    size = half // count
    copies = []
    for h, (ref, first) in enumerate(((own_ref, core * half), (other_ref, (1 - core) * half))):
        for q in range(count):
            for l in range(q * size, (q + 1) * size):
                buffer[h * half + l] = block_ref[first + l] + strength * ref[l]
            copies.append(
                pltpu.make_async_copy(
                    buffer.at[pl.ds(h * half + q * size, size)],
                    out_ref.at[0, pl.ds(first + q * size, size)],
                    sems.at[h * count + q],
                )
            )
            copies[-1].start()
    for copy in copies:
        copy.wait()


def call(kernel, ins, outs, scratch=(), flops=0):
    return pl.pallas_call(
        kernel,
        out_shape=outs,
        in_specs=[pl.BlockSpec(memory_space=pl.ANY if s is HBM else s) for _, s in ins],
        out_specs=jax.tree.map(
            lambda o: pl.BlockSpec(memory_space=VMEM if isinstance(o, pl.MemoryRef) else pl.ANY),
            outs,
            is_leaf=lambda o: isinstance(o, (pl.MemoryRef, jax.ShapeDtypeStruct)),
        ),
        scratch_shapes=scratch,
        cost_estimate=pl.CostEstimate(flops=flops, transcendentals=0, bytes_accessed=0),
    )(*[pltpu.with_memory_space_constraint(x, VMEM) if s is VMEM else x for x, s in ins])


def solution(mesh):
    count_x, count_y, count_v = (mesh.shape[a] for a in ("gx", "gy", "var"))
    ranks = count_x * count_y
    for count in (count_x, count_y, count_v):
        assert count & (count - 1) == 0

    def swap(value, bits, bits_v=0):
        bits = bits * count_v + bits_v
        pairs = [(i, i ^ bits) for i in range(ranks * count_v)]
        return lax.ppermute(value, ("gx", "gy", "var"), pairs)

    core = count_y

    bits_x = [count_y << b for b in range(1, count_x.bit_length() - 1)]
    bits_y = [1 << b for b in range(count_y.bit_length() - 1)]
    stages = []
    for b in range(max(len(bits_x), len(bits_y))):
        bx, by = bits_x[b : b + 1], bits_y[b : b + 1]
        stages.append([bits | core * ((bits + bits // (2 * core)) % 2) for bits in bx + by + [x | y for x in bx for y in by]])

    def nudge(field, drive, keep_count, level_class, height_table):
        _, levels, rows, columns = field.shape
        modes = drive.shape[-1]
        half = levels // 2
        total_x, total_y = rows * count_x, columns * count_y
        assert columns == LANES and levels % 4 == 0 and half * modes % LANES == 0 and modes % 8 == 0
        table_x = cosine_table(total_x, modes).reshape(count_x, rows, modes)
        table_y = np.zeros((count_y, columns, LANES), np.float32)
        table_y[:, :, :modes] = cosine_table(total_y, modes).reshape(count_y, columns, modes)
        tx_t = split_table(table_x.transpose(0, 2, 1) / np.float32(total_x * total_y), 2)
        ty = split_table(table_y, 1)
        tx = split_table(table_x, 2)
        ty_t = split_table(table_y.transpose(0, 2, 1), 1)
        packed = pltpu.VMEM((modes, half * modes), jnp.float32)
        cube = pltpu.VMEM((levels, rows, columns), jnp.float32)
        half_cube = pltpu.VMEM((half, rows, columns), jnp.float32)
        dma = pltpu.SemaphoreType.DMA
        like = lambda table: pltpu.VMEM(table.shape[1:], table.dtype)

        block, send, tx_t, ty = call(
            send_kernel,
            [(field, HBM), (jnp.asarray(tx_t), HBM), (jnp.asarray(ty), HBM)],
            (cube, packed, like(tx_t), like(ty)),
            [dma((5,))],
        )
        keep = call(keep_kernel, [(x, VMEM) for x in (block, tx_t, ty)], packed, flops=10**9)
        total = keep + swap(send, core)
        goal, mask, lift, tx, ty_t = call(
            prepare_kernel,
            [
                (total, VMEM),
                (keep_count, SMEM),
                (level_class, SMEM),
                (height_table, SMEM),
                (drive, HBM),
                (jnp.asarray(tx), HBM),
                (jnp.asarray(ty_t), HBM),
            ],
            (
                packed,
                packed,
                pltpu.VMEM((levels, LANES), jnp.float32),
                like(tx),
                like(ty_t),
            ),
            [pltpu.VMEM((half, modes, modes), jnp.float32), dma((3,))],
            flops=10**9,
        )
        parts = [total]
        for stage in stages:
            if len(parts) > 1:
                parts = [sum(parts[1:], parts[0])]
            parts = parts + [swap(parts[0], bits) for bits in stage]
        delta, energy = call(
            settle_kernel, [(x, VMEM) for x in (goal, mask, *parts)], (packed, pltpu.VMEM((8, LANES), jnp.float32))
        )
        energy = energy + swap(energy, core)
        shared = swap(delta, core)
        own, other = (
            call(
                functools.partial(inverse_kernel, which),
                [(x, VMEM) for x in (part, lift, tx, ty_t)],
                half_cube,
                flops=10**9,
            )
            for which, part in ((0, delta), (1, shared))
        )
        last = jnp.zeros_like(energy)
        for b in range(count_v.bit_length() - 1):
            energy = energy + last
            last = swap(energy, core, 1 << b)
        return call(
            finish_kernel,
            [(x, VMEM) for x in (energy, last, block, own, other)],
            jax.ShapeDtypeStruct(field.shape, jnp.float32),
            [pltpu.VMEM((levels, rows, columns), jnp.float32), dma((4,))],
        )

    return jax.shard_map(
        nudge,
        mesh=mesh,
        in_specs=(P("var", None, "gx", "gy"), P("var", None, None, None), P(), P(), P()),
        out_specs=P("var", None, "gx", "gy"),
        check_vma=False,
    )
```

profile of v0, /device:TPU:0, one launch (start us, length us, event | category | flops | bytes accessed | tf_op | source)
XLA Modules:
  0.0 21.9 jit_solution(2780315930665891277)
XLA Ops:
  0.0 1.7 %shard_map.91 = (f32[32,64,128]{2,1,0:T(8,128)S(1)}, f32[40,640]{1,0:T(8,128)S(1)}, bf16[80,128]{1,0:T(8,128)(2,1)S(1)}, bf16[256,256]{1,0:T(8,128)(2,1)S(1)}) custom-call(f32[1,32,64,128]{3,2,1,0:T(8,128)} %field_ref.1, bf16[4,80,128]{2,1,0:T(8,128)(2,1)} %constant.8.clone.tx_ref, bf16[2,256,256]{2,1,0:T(8,128)(2,1)} %constant.9.clone.ty_ref), custom_call_target="tpu_custom_call" | custom-call | tf_op jit(solution)/shard_map/pallas_call | solution.py:254
  1.7 0.6 %collective-permute-start = (f32[40,640]{1,0:T(8,128)S(1)}, f32[40,640]{1,0:T(8,128)S(1)}, u32[]{:S(2)}, u32[]{:S(2)}) collective-permute-start(f32[40,640]{1,0:T(8,128)S(1)} %get-tuple-element.19), channel_id=1, source_target_pairs={{0,8},{1,9},{2,10},{3,11},{4,12},{5,13},{6,14},{7,15},{8,0},{9,1},... | collective-permute-start | bytes 307208 | tf_op jit(solution)/shard_map/ppermute | solution.py:277
  2.2 0.5 %shard_map.92 = f32[40,640]{1,0:T(8,128)S(1)} custom-call(f32[32,64,128]{2,1,0:T(8,128)S(1)} %get-tuple-element.16.block_ref, bf16[80,128]{1,0:T(8,128)(2,1)S(1)} %get-tuple-element.17.tx_ref, bf16[256,256]{1,0:T(8,128)(2,1)S(1)} %get-tuple-element.18.ty_ref), custom_call_target="tpu_custom_call" | custom-call | flops 1000000000 | tf_op jit(solution)/shard_map/pallas_call | solution.py:254
  2.7 0.5 %collective-permute-done = f32[40,640]{1,0:T(8,128)S(1)} collective-permute-done((f32[40,640]{1,0:T(8,128)S(1)}, f32[40,640]{1,0:T(8,128)S(1)}, u32[]{:S(2)}, u32[]{:S(2)}) %collective-permute-start) | collective-permute-done | bytes 102432 | tf_op jit(solution)/shard_map/ppermute | solution.py:277
  3.2 3.9 %collective-permute-start.3 = (f32[40,640]{1,0:T(8,128)S(1)}, f32[40,640]{1,0:T(8,128)S(1)}, u32[]{:S(2)}, u32[]{:S(2)}) collective-permute-start(f32[40,640]{1,0:T(8,128)S(1)} %add.9._.own_ref), channel_id=1, source_target_pairs={{0,20},{1,21},{2,22},{3,23},{4,16},{5,17},{6,18},{7,19},{8,28},{9,... | collective-permute-start | bytes 307208 | tf_op jit(solution)/shard_map/ppermute | solution.py:277
  7.1 0.0 collective-permute-start.2
  7.1 0.4 %collective-permute-start.1 = (f32[40,640]{1,0:T(8,128)S(1)}, f32[40,640]{1,0:T(8,128)S(1)}, u32[]{:S(2)}, u32[]{:S(2)}) collective-permute-start(f32[40,640]{1,0:T(8,128)S(1)} %add.9._.own_ref), channel_id=1, source_target_pairs={{0,24},{1,25},{2,26},{3,27},{4,28},{5,29},{6,30},{7,31},{8,16},{9,... | collective-permute-start | bytes 307208 | tf_op jit(solution)/shard_map/ppermute | solution.py:277
  7.4 1.9 %shard_map.93 = (f32[40,640]{1,0:T(8,128)S(1)}, f32[40,640]{1,0:T(8,128)S(1)}, f32[32,128]{1,0:T(8,128)S(1)}, bf16[128,80]{1,0:T(8,128)(2,1)S(1)}, bf16[256,256]{1,0:T(8,128)(2,1)S(1)}) custom-call(f32[40,640]{1,0:T(8,128)S(1)} %add.9._.own_ref, s32[32]{0:T(128)} %keep_count_ref.1, s32[32]{0:T(128)} %class_ref.1, f32[8]{0:T(128)} %height_ref.1, ...), custom_call_target="tpu_custom_call" | custom-call | flops 1000000000 | tf_op jit(solution)/shard_map/pallas_call | solution.py:254
  9.3 1.2 %collective-permute-done.3.rest_2_ = f32[40,640]{1,0:T(8,128)S(1)} collective-permute-done((f32[40,640]{1,0:T(8,128)S(1)}, f32[40,640]{1,0:T(8,128)S(1)}, u32[]{:S(2)}, u32[]{:S(2)}) %collective-permute-start.3) | collective-permute-done | bytes 102432 | tf_op jit(solution)/shard_map/ppermute | solution.py:277
  10.5 1.7 %collective-permute-done.2.rest_1_ = f32[40,640]{1,0:T(8,128)S(1)} collective-permute-done((f32[40,640]{1,0:T(8,128)S(1)}, f32[40,640]{1,0:T(8,128)S(1)}, u32[]{:S(2)}, u32[]{:S(2)}) %collective-permute-start.2) | collective-permute-done | bytes 102432 | tf_op jit(solution)/shard_map/ppermute | solution.py:277
  12.2 0.0 collective-permute-done.1.rest_0_
  12.2 0.1 shard_map.94
  12.3 0.3 %collective-permute-start.7 = (f32[40,640]{1,0:T(8,128)S(1)}, f32[40,640]{1,0:T(8,128)S(1)}, u32[]{:S(2)}, u32[]{:S(2)}) collective-permute-start(f32[40,640]{1,0:T(8,128)S(1)} %get-tuple-element.23.delta_ref), channel_id=1, source_target_pairs={{0,8},{1,9},{2,10},{3,11},{4,12},{5,13},{6,14},{7,15},{8,0},{9,1},... | collective-permute-start | bytes 307208 | tf_op jit(solution)/shard_map/ppermute | solution.py:277
  12.7 0.2 %collective-permute-start.4 = (f32[8,128]{1,0:T(8,128)S(1)}, f32[8,128]{1,0:T(8,128)S(1)}, u32[]{:S(2)}, u32[]{:S(2)}) collective-permute-start(f32[8,128]{1,0:T(8,128)S(1)} %get-tuple-element.22), channel_id=1, source_target_pairs={{0,8},{1,9},{2,10},{3,11},{4,12},{5,13},{6,14},{7,15},{8,0},{9,1},... | collective-permute-start | bytes 12296 | tf_op jit(solution)/shard_map/ppermute | solution.py:277
  12.9 0.9 %collective-permute-done.4 = f32[8,128]{1,0:T(8,128)S(1)} collective-permute-done((f32[8,128]{1,0:T(8,128)S(1)}, f32[8,128]{1,0:T(8,128)S(1)}, u32[]{:S(2)}, u32[]{:S(2)}) %collective-permute-start.4) | collective-permute-done | bytes 4128 | tf_op jit(solution)/shard_map/ppermute | solution.py:277
  13.8 1.4 %collective-permute-start.5 = (f32[8,128]{1,0:T(8,128)S(1)}, f32[8,128]{1,0:T(8,128)S(1)}, u32[]{:S(2)}, u32[]{:S(2)}) collective-permute-start(f32[8,128]{1,0:T(8,128)S(1)} %add.10), channel_id=1, source_target_pairs={{0,9},{1,8},{2,11},{3,10},{4,13},{5,12},{6,15},{7,14},{8,1},{9,0},... | collective-permute-start | bytes 12296 | tf_op jit(solution)/shard_map/ppermute | solution.py:277
  15.3 0.6 %shard_map.95.own_ref = f32[16,64,128]{2,1,0:T(8,128)S(1)} custom-call(f32[40,640]{1,0:T(8,128)S(1)} %get-tuple-element.23.delta_ref, f32[32,128]{1,0:T(8,128)S(1)} %get-tuple-element.24.lift_ref, bf16[128,80]{1,0:T(8,128)(2,1)S(1)} %get-tuple-element.25.tx_ref, bf16[256,256]{1,0:T(8,128)(2,1)S(1)} %get-tuple-element.26.ty_ref), custom_call_target="tpu_custom_call" | custom-call | flops 1000000000 | tf_op jit(solution)/shard_map/pallas_call | solution.py:254
  15.8 1.0 %collective-permute-done.5 = f32[8,128]{1,0:T(8,128)S(1)} collective-permute-done((f32[8,128]{1,0:T(8,128)S(1)}, f32[8,128]{1,0:T(8,128)S(1)}, u32[]{:S(2)}, u32[]{:S(2)}) %collective-permute-start.5) | collective-permute-done | bytes 4128 | tf_op jit(solution)/shard_map/ppermute | solution.py:277
  16.9 2.4 %collective-permute-start.6 = (f32[8,128]{1,0:T(8,128)S(1)}, f32[8,128]{1,0:T(8,128)S(1)}, u32[]{:S(2)}, u32[]{:S(2)}) collective-permute-start(f32[8,128]{1,0:T(8,128)S(1)} %add.11.energy_ref), channel_id=1, source_target_pairs={{0,10},{1,11},{2,8},{3,9},{4,14},{5,15},{6,12},{7,13},{8,2},{9,3},... | collective-permute-start | bytes 12296 | tf_op jit(solution)/shard_map/ppermute | solution.py:277
  19.3 0.0 collective-permute-done.7.delta_ref
  19.3 0.6 %shard_map.96.other_ref = f32[16,64,128]{2,1,0:T(8,128)S(1)} custom-call(f32[40,640]{1,0:T(8,128)S(1)} %collective-permute-done.7.delta_ref, f32[32,128]{1,0:T(8,128)S(1)} %get-tuple-element.24.lift_ref, bf16[128,80]{1,0:T(8,128)(2,1)S(1)} %get-tuple-element.25.tx_ref, bf16[256,256]{1,0:T(8,128)(2,1)S(1)} %get-tuple-element.26.ty_ref), custom_call_target="tpu_custom_call" | custom-call | flops 1000000000 | tf_op jit(solution)/shard_map/pallas_call | solution.py:254
  19.9 0.9 %collective-permute-done.6.last_ref = f32[8,128]{1,0:T(8,128)S(1)} collective-permute-done((f32[8,128]{1,0:T(8,128)S(1)}, f32[8,128]{1,0:T(8,128)S(1)}, u32[]{:S(2)}, u32[]{:S(2)}) %collective-permute-start.6) | collective-permute-done | bytes 4128 | tf_op jit(solution)/shard_map/ppermute | solution.py:277
  20.8 1.2 %shard_map.97 = f32[1,32,64,128]{3,2,1,0:T(8,128)} custom-call(f32[8,128]{1,0:T(8,128)S(1)} %add.11.energy_ref, f32[8,128]{1,0:T(8,128)S(1)} %collective-permute-done.6.last_ref, f32[32,64,128]{2,1,0:T(8,128)S(1)} %get-tuple-element.16.block_ref, f32[16,64,128]{2,1,0:T(8,128)S(1)} %shard_map.95.own_ref, f32[16,64,128]{2,1,0:T(8,128)S(1)} %shard_map.96.other_ref), custom_call_target="tpu_custom_call" | custom-call | tf_op jit(solution)/shard_map/pallas_call | solution.py:254
  (3 shorter events, 0.0 us)
Async XLA Ops:
  1.7 1.5 %collective-permute-start = (f32[40,640]{1,0:T(8,128)S(1)}, f32[40,640]{1,0:T(8,128)S(1)}, u32[]{:S(2)}, u32[]{:S(2)}) collective-permute-start(f32[40,640]{1,0:T(8,128)S(1)} %get-tuple-element.19), channel_id=1, source_target_pairs={{0,8},{1,9},{2,10},{3,11},{4,12},{5,13},{6,14},{7,15},{8,0},{9,1},... | collective-permute-start | bytes 307208 | tf_op jit(solution)/shard_map/ppermute | solution.py:277
  3.2 7.3 %collective-permute-start.3 = (f32[40,640]{1,0:T(8,128)S(1)}, f32[40,640]{1,0:T(8,128)S(1)}, u32[]{:S(2)}, u32[]{:S(2)}) collective-permute-start(f32[40,640]{1,0:T(8,128)S(1)} %add.9._.own_ref), channel_id=1, source_target_pairs={{0,20},{1,21},{2,22},{3,23},{4,16},{5,17},{6,18},{7,19},{8,28},{9,... | collective-permute-start | bytes 307208 | tf_op jit(solution)/shard_map/ppermute | solution.py:277
  7.1 5.2 %collective-permute-start.2 = (f32[40,640]{1,0:T(8,128)S(1)}, f32[40,640]{1,0:T(8,128)S(1)}, u32[]{:S(2)}, u32[]{:S(2)}) collective-permute-start(f32[40,640]{1,0:T(8,128)S(1)} %add.9._.own_ref), channel_id=1, source_target_pairs={{0,12},{1,13},{2,14},{3,15},{4,8},{5,9},{6,10},{7,11},{8,4},{9,5},... | collective-permute-start | bytes 307208 | tf_op jit(solution)/shard_map/ppermute | solution.py:277
  7.1 5.2 %collective-permute-start.1 = (f32[40,640]{1,0:T(8,128)S(1)}, f32[40,640]{1,0:T(8,128)S(1)}, u32[]{:S(2)}, u32[]{:S(2)}) collective-permute-start(f32[40,640]{1,0:T(8,128)S(1)} %add.9._.own_ref), channel_id=1, source_target_pairs={{0,24},{1,25},{2,26},{3,27},{4,28},{5,29},{6,30},{7,31},{8,16},{9,... | collective-permute-start | bytes 307208 | tf_op jit(solution)/shard_map/ppermute | solution.py:277
  12.3 7.0 %collective-permute-start.7 = (f32[40,640]{1,0:T(8,128)S(1)}, f32[40,640]{1,0:T(8,128)S(1)}, u32[]{:S(2)}, u32[]{:S(2)}) collective-permute-start(f32[40,640]{1,0:T(8,128)S(1)} %get-tuple-element.23.delta_ref), channel_id=1, source_target_pairs={{0,8},{1,9},{2,10},{3,11},{4,12},{5,13},{6,14},{7,15},{8,0},{9,1},... | collective-permute-start | bytes 307208 | tf_op jit(solution)/shard_map/ppermute | solution.py:277
  12.7 1.2 %collective-permute-start.4 = (f32[8,128]{1,0:T(8,128)S(1)}, f32[8,128]{1,0:T(8,128)S(1)}, u32[]{:S(2)}, u32[]{:S(2)}) collective-permute-start(f32[8,128]{1,0:T(8,128)S(1)} %get-tuple-element.22), channel_id=1, source_target_pairs={{0,8},{1,9},{2,10},{3,11},{4,12},{5,13},{6,14},{7,15},{8,0},{9,1},... | collective-permute-start | bytes 12296 | tf_op jit(solution)/shard_map/ppermute | solution.py:277
  13.8 3.0 %collective-permute-start.5 = (f32[8,128]{1,0:T(8,128)S(1)}, f32[8,128]{1,0:T(8,128)S(1)}, u32[]{:S(2)}, u32[]{:S(2)}) collective-permute-start(f32[8,128]{1,0:T(8,128)S(1)} %add.10), channel_id=1, source_target_pairs={{0,9},{1,8},{2,11},{3,10},{4,13},{5,12},{6,15},{7,14},{8,1},{9,0},... | collective-permute-start | bytes 12296 | tf_op jit(solution)/shard_map/ppermute | solution.py:277
  16.9 3.9 %collective-permute-start.6 = (f32[8,128]{1,0:T(8,128)S(1)}, f32[8,128]{1,0:T(8,128)S(1)}, u32[]{:S(2)}, u32[]{:S(2)}) collective-permute-start(f32[8,128]{1,0:T(8,128)S(1)} %add.11.energy_ref), channel_id=1, source_target_pairs={{0,10},{1,11},{2,8},{3,9},{4,14},{5,15},{6,12},{7,13},{8,2},{9,3},... | collective-permute-start | bytes 12296 | tf_op jit(solution)/shard_map/ppermute | solution.py:277
where the time goes:
time: 22.1 us; the launch traced here: 21.9 us
  starting transfers between devices  9.23 us (42%)
  Pallas kernels  6.36 us (29%)
  waiting for transfers between devices  6.3 us (29%)
    ppermute x8, starting transfers between devices, swap(): return lax.ppermute(value, ('gx', 'gy', 'var'), pairs)  9.23 us
    pallas_call x7, Pallas kernels, call(): pl.pallas_call(kernel, out_shape=outs, in_specs=[pl.BlockSpec(memory_spac...  6.36 us
    ppermute x8, waiting for transfers between devices, swap(): return lax.ppermute(value, ('gx', 'gy', 'var'), pairs)  6.3 us
  transfers between devices with their start and end apart: 8, of which 6 were waited for; matrix products, arithmetic and copies ran while one was open for 0% of the time, Pallas kernels for 16%

commit v1 on v0

--- a/solution.py
+++ b/solution.py
@@ -45,8 +45,8 @@
 def split_table(table, axis):
     high = table.astype(jnp.bfloat16)
     low = (table - high.astype(np.float32)).astype(jnp.bfloat16)
-    top = np.concatenate([high, high], axis=axis)
-    return np.concatenate([top, np.concatenate([low, np.zeros_like(low)], axis=axis)], axis=3 - axis)
+    both = np.concatenate([high, low], axis=3 - axis)
+    return np.concatenate([both, both], axis=axis)
 
 
 def owned_half():
@@ -85,12 +85,13 @@
     return pieces
 
 
-def transform(block, tx, ty, modes):
+def transform(block, tx, ty_ref, modes, ready=lambda: None):
     wide = stack_split(jnp.concatenate(block, axis=1), 0)
     both = dot(tx, wide)
     part = both[:modes] + both[modes:]
     tall = jnp.concatenate([part[:, l * LANES : (l + 1) * LANES] for l in range(len(block))], axis=0)
-    both = dot(stack_split(tall, 1), ty)
+    ready()
+    both = dot(stack_split(tall, 1), ty_ref[...])
     coeff = both[:, :LANES] + both[:, LANES:]
     return [coeff[l * modes : (l + 1) * modes] for l in range(len(block))]
 
@@ -103,30 +104,24 @@
 def send_kernel(field_ref, tx_ref, ty_ref, block_ref, send_ref, tx, ty, sems):
     half = block_ref.shape[0] // 2
     modes = send_ref.shape[0]
-    at_x, at_y = lax.axis_index("gx"), lax.axis_index("gy")
-    core = owned_half()
-    first = (1 - core) * half
-    starts = [first, core * half]
-    copies = [
-        pltpu.make_async_copy(tx_ref.at[at_x], tx, sems.at[0]),
-        pltpu.make_async_copy(ty_ref.at[at_y], ty, sems.at[1]),
-    ]
-    for q, (start, size) in enumerate(zip(starts, (half, half))):
-        rows = pl.ds(start, size)
-        copies.append(
-            pltpu.make_async_copy(field_ref.at[0, rows], block_ref.at[rows], sems.at[2 + q])
-        )
-    for copy in copies:
+    owned = owned_half()
+    first = (1 - owned) * half
+
+    def levels_copy(start, sem):
+        rows = pl.ds(start, half)
+        return pltpu.make_async_copy(field_ref.at[0, rows], block_ref.at[rows], sem)
+
+    sent = levels_copy(first, sems.at[0])
+    kept = levels_copy(owned * half, sems.at[1])
+    tx_copy = pltpu.make_async_copy(tx_ref.at[lax.axis_index("gx")], tx, sems.at[2])
+    ty_copy = pltpu.make_async_copy(ty_ref.at[lax.axis_index("gy")], ty, sems.at[3])
+    for copy in (sent, tx_copy, ty_copy, kept):
         copy.start()
-    copies[0].wait()
-    copies[1].wait()
-    pieces = []
-    for q in range(1):
-        copies[2 + q].wait()
-        levels = [block_ref[first + l] for l in range(half)]
-        pieces += transform(levels, tx[...], ty[...], modes)
-    store_packed(send_ref, pieces, modes)
-    copies[3].wait()
+    tx_copy.wait()
+    sent.wait()
+    levels = [block_ref[first + l] for l in range(half)]
+    store_packed(send_ref, transform(levels, tx[...], ty, modes, ty_copy.wait), modes)
+    kept.wait()
 
 
 def keep_kernel(block_ref, tx_ref, ty_ref, keep_ref):
@@ -134,7 +129,7 @@
     modes = keep_ref.shape[0]
     first = owned_half() * half
     levels = [block_ref[first + l] for l in range(half)]
-    store_packed(keep_ref, transform(levels, tx_ref[...], ty_ref[...], modes), modes)
+    store_packed(keep_ref, transform(levels, tx_ref[...], ty_ref, modes), modes)
 
 
 def prepare_kernel(
@@ -308,7 +303,7 @@
             send_kernel,
             [(field, HBM), (jnp.asarray(tx_t), HBM), (jnp.asarray(ty), HBM)],
             (cube, packed, like(tx_t), like(ty)),
-            [dma((5,))],
+            [dma((4,))],
         )
         keep = call(keep_kernel, [(x, VMEM) for x in (block, tx_t, ty)], packed, flops=10**9)
         total = keep + swap(send, core)
@@ -339,7 +334,9 @@
                 parts = [sum(parts[1:], parts[0])]
             parts = parts + [swap(parts[0], bits) for bits in stage]
         delta, energy = call(
-            settle_kernel, [(x, VMEM) for x in (goal, mask, *parts)], (packed, pltpu.VMEM((8, LANES), jnp.float32))
+            settle_kernel,
+            [(x, VMEM) for x in (goal, mask, *parts)],
+            (packed, pltpu.VMEM((8, LANES), jnp.float32)),
         )
         energy = energy + swap(energy, core)
         shared = swap(delta, core)

time: 22.1 us -> 22.1 us (level)
  no operation moved by 1% of the time
where the time goes in v1:
time: 22.1 us; the launch traced here: 21.9 us
  starting transfers between devices  9.23 us (42%)
  Pallas kernels  6.32 us (29%)
  waiting for transfers between devices  6.32 us (29%)
    ppermute x8, starting transfers between devices, swap(): return lax.ppermute(value, ('gx', 'gy', 'var'), pairs)  9.23 us
    ppermute x8, waiting for transfers between devices, swap(): return lax.ppermute(value, ('gx', 'gy', 'var'), pairs)  6.32 us
    pallas_call x7, Pallas kernels, call(): pl.pallas_call(kernel, out_shape=outs, in_specs=[pl.BlockSpec(memory_spac...  6.32 us
  transfers between devices with their start and end apart: 8, of which 6 were waited for; matrix products, arithmetic and copies ran while one was open for 0% of the time, Pallas kernels for 16%

profile of v1, /device:TPU:0, one launch (start us, length us, event | category | flops | bytes accessed | tf_op | source)
XLA Modules:
  0.0 21.9 jit_solution(7525972526870687946)
XLA Ops:
  0.0 1.6 %shard_map.91 = (f32[32,64,128]{2,1,0:T(8,128)S(1)}, f32[40,640]{1,0:T(8,128)S(1)}, bf16[80,128]{1,0:T(8,128)(2,1)S(1)}, bf16[256,256]{1,0:T(8,128)(2,1)S(1)}) custom-call(f32[1,32,64,128]{3,2,1,0:T(8,128)} %field_ref.1, bf16[4,80,128]{2,1,0:T(8,128)(2,1)} %constant.8.clone.tx_ref, bf16[2,256,256]{2,1,0:T(8,128)(2,1)} %constant.9.clone.ty_ref), custom_call_target="tpu_custom_call" | custom-call | tf_op jit(solution)/shard_map/pallas_call | solution.py:249
  1.7 0.6 %collective-permute-start = (f32[40,640]{1,0:T(8,128)S(1)}, f32[40,640]{1,0:T(8,128)S(1)}, u32[]{:S(2)}, u32[]{:S(2)}) collective-permute-start(f32[40,640]{1,0:T(8,128)S(1)} %get-tuple-element.19), channel_id=1, source_target_pairs={{0,8},{1,9},{2,10},{3,11},{4,12},{5,13},{6,14},{7,15},{8,0},{9,1},... | collective-permute-start | bytes 307208 | tf_op jit(solution)/shard_map/ppermute | solution.py:272
  2.2 0.5 %shard_map.92 = f32[40,640]{1,0:T(8,128)S(1)} custom-call(f32[32,64,128]{2,1,0:T(8,128)S(1)} %get-tuple-element.16.block_ref, bf16[80,128]{1,0:T(8,128)(2,1)S(1)} %get-tuple-element.17.tx_ref, bf16[256,256]{1,0:T(8,128)(2,1)S(1)} %get-tuple-element.18.ty_ref), custom_call_target="tpu_custom_call" | custom-call | flops 1000000000 | tf_op jit(solution)/shard_map/pallas_call | solution.py:249
  2.7 0.5 %collective-permute-done = f32[40,640]{1,0:T(8,128)S(1)} collective-permute-done((f32[40,640]{1,0:T(8,128)S(1)}, f32[40,640]{1,0:T(8,128)S(1)}, u32[]{:S(2)}, u32[]{:S(2)}) %collective-permute-start) | collective-permute-done | bytes 102432 | tf_op jit(solution)/shard_map/ppermute | solution.py:272
  3.2 3.9 %collective-permute-start.3 = (f32[40,640]{1,0:T(8,128)S(1)}, f32[40,640]{1,0:T(8,128)S(1)}, u32[]{:S(2)}, u32[]{:S(2)}) collective-permute-start(f32[40,640]{1,0:T(8,128)S(1)} %add.9._.own_ref), channel_id=1, source_target_pairs={{0,20},{1,21},{2,22},{3,23},{4,16},{5,17},{6,18},{7,19},{8,28},{9,... | collective-permute-start | bytes 307208 | tf_op jit(solution)/shard_map/ppermute | solution.py:272
  7.0 0.0 collective-permute-start.2
  7.0 0.3 %collective-permute-start.1 = (f32[40,640]{1,0:T(8,128)S(1)}, f32[40,640]{1,0:T(8,128)S(1)}, u32[]{:S(2)}, u32[]{:S(2)}) collective-permute-start(f32[40,640]{1,0:T(8,128)S(1)} %add.9._.own_ref), channel_id=1, source_target_pairs={{0,24},{1,25},{2,26},{3,27},{4,28},{5,29},{6,30},{7,31},{8,16},{9,... | collective-permute-start | bytes 307208 | tf_op jit(solution)/shard_map/ppermute | solution.py:272
  7.4 1.9 %shard_map.93 = (f32[40,640]{1,0:T(8,128)S(1)}, f32[40,640]{1,0:T(8,128)S(1)}, f32[32,128]{1,0:T(8,128)S(1)}, bf16[128,80]{1,0:T(8,128)(2,1)S(1)}, bf16[256,256]{1,0:T(8,128)(2,1)S(1)}) custom-call(f32[40,640]{1,0:T(8,128)S(1)} %add.9._.own_ref, s32[32]{0:T(128)} %keep_count_ref.1, s32[32]{0:T(128)} %class_ref.1, f32[8]{0:T(128)} %height_ref.1, ...), custom_call_target="tpu_custom_call" | custom-call | flops 1000000000 | tf_op jit(solution)/shard_map/pallas_call | solution.py:249
  9.3 1.2 %collective-permute-done.3.rest_2_ = f32[40,640]{1,0:T(8,128)S(1)} collective-permute-done((f32[40,640]{1,0:T(8,128)S(1)}, f32[40,640]{1,0:T(8,128)S(1)}, u32[]{:S(2)}, u32[]{:S(2)}) %collective-permute-start.3) | collective-permute-done | bytes 102432 | tf_op jit(solution)/shard_map/ppermute | solution.py:272
  10.5 1.7 %collective-permute-done.2.rest_1_ = f32[40,640]{1,0:T(8,128)S(1)} collective-permute-done((f32[40,640]{1,0:T(8,128)S(1)}, f32[40,640]{1,0:T(8,128)S(1)}, u32[]{:S(2)}, u32[]{:S(2)}) %collective-permute-start.2) | collective-permute-done | bytes 102432 | tf_op jit(solution)/shard_map/ppermute | solution.py:272
  12.2 0.0 collective-permute-done.1.rest_0_
  12.2 0.1 shard_map.94
  12.3 0.4 %collective-permute-start.7 = (f32[40,640]{1,0:T(8,128)S(1)}, f32[40,640]{1,0:T(8,128)S(1)}, u32[]{:S(2)}, u32[]{:S(2)}) collective-permute-start(f32[40,640]{1,0:T(8,128)S(1)} %get-tuple-element.23.delta_ref), channel_id=1, source_target_pairs={{0,8},{1,9},{2,10},{3,11},{4,12},{5,13},{6,14},{7,15},{8,0},{9,1},... | collective-permute-start | bytes 307208 | tf_op jit(solution)/shard_map/ppermute | solution.py:272
  12.6 0.2 %collective-permute-start.4 = (f32[8,128]{1,0:T(8,128)S(1)}, f32[8,128]{1,0:T(8,128)S(1)}, u32[]{:S(2)}, u32[]{:S(2)}) collective-permute-start(f32[8,128]{1,0:T(8,128)S(1)} %get-tuple-element.22), channel_id=1, source_target_pairs={{0,8},{1,9},{2,10},{3,11},{4,12},{5,13},{6,14},{7,15},{8,0},{9,1},... | collective-permute-start | bytes 12296 | tf_op jit(solution)/shard_map/ppermute | solution.py:272
  12.9 0.9 %collective-permute-done.4 = f32[8,128]{1,0:T(8,128)S(1)} collective-permute-done((f32[8,128]{1,0:T(8,128)S(1)}, f32[8,128]{1,0:T(8,128)S(1)}, u32[]{:S(2)}, u32[]{:S(2)}) %collective-permute-start.4) | collective-permute-done | bytes 4128 | tf_op jit(solution)/shard_map/ppermute | solution.py:272
  13.8 1.4 %collective-permute-start.5 = (f32[8,128]{1,0:T(8,128)S(1)}, f32[8,128]{1,0:T(8,128)S(1)}, u32[]{:S(2)}, u32[]{:S(2)}) collective-permute-start(f32[8,128]{1,0:T(8,128)S(1)} %add.10), channel_id=1, source_target_pairs={{0,9},{1,8},{2,11},{3,10},{4,13},{5,12},{6,15},{7,14},{8,1},{9,0},... | collective-permute-start | bytes 12296 | tf_op jit(solution)/shard_map/ppermute | solution.py:272
  15.2 0.6 %shard_map.95.own_ref = f32[16,64,128]{2,1,0:T(8,128)S(1)} custom-call(f32[40,640]{1,0:T(8,128)S(1)} %get-tuple-element.23.delta_ref, f32[32,128]{1,0:T(8,128)S(1)} %get-tuple-element.24.lift_ref, bf16[128,80]{1,0:T(8,128)(2,1)S(1)} %get-tuple-element.25.tx_ref, bf16[256,256]{1,0:T(8,128)(2,1)S(1)} %get-tuple-element.26.ty_ref), custom_call_target="tpu_custom_call" | custom-call | flops 1000000000 | tf_op jit(solution)/shard_map/pallas_call | solution.py:249
  15.8 1.0 %collective-permute-done.5 = f32[8,128]{1,0:T(8,128)S(1)} collective-permute-done((f32[8,128]{1,0:T(8,128)S(1)}, f32[8,128]{1,0:T(8,128)S(1)}, u32[]{:S(2)}, u32[]{:S(2)}) %collective-permute-start.5) | collective-permute-done | bytes 4128 | tf_op jit(solution)/shard_map/ppermute | solution.py:272
  16.8 2.4 %collective-permute-start.6 = (f32[8,128]{1,0:T(8,128)S(1)}, f32[8,128]{1,0:T(8,128)S(1)}, u32[]{:S(2)}, u32[]{:S(2)}) collective-permute-start(f32[8,128]{1,0:T(8,128)S(1)} %add.11.energy_ref), channel_id=1, source_target_pairs={{0,10},{1,11},{2,8},{3,9},{4,14},{5,15},{6,12},{7,13},{8,2},{9,3},... | collective-permute-start | bytes 12296 | tf_op jit(solution)/shard_map/ppermute | solution.py:272
  19.3 0.0 collective-permute-done.7.delta_ref
  19.3 0.6 %shard_map.96.other_ref = f32[16,64,128]{2,1,0:T(8,128)S(1)} custom-call(f32[40,640]{1,0:T(8,128)S(1)} %collective-permute-done.7.delta_ref, f32[32,128]{1,0:T(8,128)S(1)} %get-tuple-element.24.lift_ref, bf16[128,80]{1,0:T(8,128)(2,1)S(1)} %get-tuple-element.25.tx_ref, bf16[256,256]{1,0:T(8,128)(2,1)S(1)} %get-tuple-element.26.ty_ref), custom_call_target="tpu_custom_call" | custom-call | flops 1000000000 | tf_op jit(solution)/shard_map/pallas_call | solution.py:249
  19.9 0.9 %collective-permute-done.6.last_ref = f32[8,128]{1,0:T(8,128)S(1)} collective-permute-done((f32[8,128]{1,0:T(8,128)S(1)}, f32[8,128]{1,0:T(8,128)S(1)}, u32[]{:S(2)}, u32[]{:S(2)}) %collective-permute-start.6) | collective-permute-done | bytes 4128 | tf_op jit(solution)/shard_map/ppermute | solution.py:272
  20.8 1.2 %shard_map.97 = f32[1,32,64,128]{3,2,1,0:T(8,128)} custom-call(f32[8,128]{1,0:T(8,128)S(1)} %add.11.energy_ref, f32[8,128]{1,0:T(8,128)S(1)} %collective-permute-done.6.last_ref, f32[32,64,128]{2,1,0:T(8,128)S(1)} %get-tuple-element.16.block_ref, f32[16,64,128]{2,1,0:T(8,128)S(1)} %shard_map.95.own_ref, f32[16,64,128]{2,1,0:T(8,128)S(1)} %shard_map.96.other_ref), custom_call_target="tpu_custom_call" | custom-call | tf_op jit(solution)/shard_map/pallas_call | solution.py:249
  (3 shorter events, 0.0 us)
Async XLA Ops:
  1.7 1.5 %collective-permute-start = (f32[40,640]{1,0:T(8,128)S(1)}, f32[40,640]{1,0:T(8,128)S(1)}, u32[]{:S(2)}, u32[]{:S(2)}) collective-permute-start(f32[40,640]{1,0:T(8,128)S(1)} %get-tuple-element.19), channel_id=1, source_target_pairs={{0,8},{1,9},{2,10},{3,11},{4,12},{5,13},{6,14},{7,15},{8,0},{9,1},... | collective-permute-start | bytes 307208 | tf_op jit(solution)/shard_map/ppermute | solution.py:272
  3.2 7.3 %collective-permute-start.3 = (f32[40,640]{1,0:T(8,128)S(1)}, f32[40,640]{1,0:T(8,128)S(1)}, u32[]{:S(2)}, u32[]{:S(2)}) collective-permute-start(f32[40,640]{1,0:T(8,128)S(1)} %add.9._.own_ref), channel_id=1, source_target_pairs={{0,20},{1,21},{2,22},{3,23},{4,16},{5,17},{6,18},{7,19},{8,28},{9,... | collective-permute-start | bytes 307208 | tf_op jit(solution)/shard_map/ppermute | solution.py:272
  7.0 5.2 %collective-permute-start.2 = (f32[40,640]{1,0:T(8,128)S(1)}, f32[40,640]{1,0:T(8,128)S(1)}, u32[]{:S(2)}, u32[]{:S(2)}) collective-permute-start(f32[40,640]{1,0:T(8,128)S(1)} %add.9._.own_ref), channel_id=1, source_target_pairs={{0,12},{1,13},{2,14},{3,15},{4,8},{5,9},{6,10},{7,11},{8,4},{9,5},... | collective-permute-start | bytes 307208 | tf_op jit(solution)/shard_map/ppermute | solution.py:272
  7.0 5.2 %collective-permute-start.1 = (f32[40,640]{1,0:T(8,128)S(1)}, f32[40,640]{1,0:T(8,128)S(1)}, u32[]{:S(2)}, u32[]{:S(2)}) collective-permute-start(f32[40,640]{1,0:T(8,128)S(1)} %add.9._.own_ref), channel_id=1, source_target_pairs={{0,24},{1,25},{2,26},{3,27},{4,28},{5,29},{6,30},{7,31},{8,16},{9,... | collective-permute-start | bytes 307208 | tf_op jit(solution)/shard_map/ppermute | solution.py:272
  12.3 7.0 %collective-permute-start.7 = (f32[40,640]{1,0:T(8,128)S(1)}, f32[40,640]{1,0:T(8,128)S(1)}, u32[]{:S(2)}, u32[]{:S(2)}) collective-permute-start(f32[40,640]{1,0:T(8,128)S(1)} %get-tuple-element.23.delta_ref), channel_id=1, source_target_pairs={{0,8},{1,9},{2,10},{3,11},{4,12},{5,13},{6,14},{7,15},{8,0},{9,1},... | collective-permute-start | bytes 307208 | tf_op jit(solution)/shard_map/ppermute | solution.py:272
  12.6 1.2 %collective-permute-start.4 = (f32[8,128]{1,0:T(8,128)S(1)}, f32[8,128]{1,0:T(8,128)S(1)}, u32[]{:S(2)}, u32[]{:S(2)}) collective-permute-start(f32[8,128]{1,0:T(8,128)S(1)} %get-tuple-element.22), channel_id=1, source_target_pairs={{0,8},{1,9},{2,10},{3,11},{4,12},{5,13},{6,14},{7,15},{8,0},{9,1},... | collective-permute-start | bytes 12296 | tf_op jit(solution)/shard_map/ppermute | solution.py:272
  13.8 3.0 %collective-permute-start.5 = (f32[8,128]{1,0:T(8,128)S(1)}, f32[8,128]{1,0:T(8,128)S(1)}, u32[]{:S(2)}, u32[]{:S(2)}) collective-permute-start(f32[8,128]{1,0:T(8,128)S(1)} %add.10), channel_id=1, source_target_pairs={{0,9},{1,8},{2,11},{3,10},{4,13},{5,12},{6,15},{7,14},{8,1},{9,0},... | collective-permute-start | bytes 12296 | tf_op jit(solution)/shard_map/ppermute | solution.py:272
  16.8 3.9 %collective-permute-start.6 = (f32[8,128]{1,0:T(8,128)S(1)}, f32[8,128]{1,0:T(8,128)S(1)}, u32[]{:S(2)}, u32[]{:S(2)}) collective-permute-start(f32[8,128]{1,0:T(8,128)S(1)} %add.11.energy_ref), channel_id=1, source_target_pairs={{0,10},{1,11},{2,8},{3,9},{4,14},{5,15},{6,12},{7,13},{8,2},{9,3},... | collective-permute-start | bytes 12296 | tf_op jit(solution)/shard_map/ppermute | solution.py:272

commit v2 on v1

--- a/solution.py
+++ b/solution.py
@@ -91,7 +91,8 @@
     part = both[:modes] + both[modes:]
     tall = jnp.concatenate([part[:, l * LANES : (l + 1) * LANES] for l in range(len(block))], axis=0)
     ready()
-    both = dot(stack_split(tall, 1), ty_ref[...])
+    table = ty_ref[...]
+    both = dot(stack_split(tall, 1), jnp.concatenate([table, table], axis=0))
     coeff = both[:, :LANES] + both[:, LANES:]
     return [coeff[l * modes : (l + 1) * modes] for l in range(len(block))]
 
@@ -223,8 +224,8 @@
     half = own_ref.shape[0]
     core = owned_half()
     energy = energy_ref[...] + last_ref[...]
-    gap = jnp.sum(energy[:1], keepdims=True)
-    model = jnp.sum(energy[1:2], keepdims=True)
+    total = jnp.sum(energy, axis=1, keepdims=True)
+    gap, model = total[:1], total[1:2]
     strength = strength_top * gap / (gap + model + epsilon)
     count = sems.shape[0] // 2
     size = half // count
@@ -240,7 +241,7 @@
                     sems.at[h * count + q],
                 )
             )
-            copies[-1].start()
+            copies[-1].start(priority=q % 2)
     for copy in copies:
         copy.wait()
 
@@ -290,7 +291,7 @@
         table_y = np.zeros((count_y, columns, LANES), np.float32)
         table_y[:, :, :modes] = cosine_table(total_y, modes).reshape(count_y, columns, modes)
         tx_t = split_table(table_x.transpose(0, 2, 1) / np.float32(total_x * total_y), 2)
-        ty = split_table(table_y, 1)
+        ty = split_table(table_y, 1)[:, :columns]
         tx = split_table(table_x, 2)
         ty_t = split_table(table_y.transpose(0, 2, 1), 1)
         packed = pltpu.VMEM((modes, half * modes), jnp.float32)

time: 22.1 us -> 22.1 us (level)
  no operation moved by 1% of the time
where the time goes in v2:
time: 22.1 us; the launch traced here: 21.9 us
  starting transfers between devices  9.23 us (42%)
  Pallas kernels  6.32 us (29%)
  waiting for transfers between devices  6.31 us (29%)
    ppermute x8, starting transfers between devices, swap(): return lax.ppermute(value, ('gx', 'gy', 'var'), pairs)  9.23 us
    pallas_call x7, Pallas kernels, call(): pl.pallas_call(kernel, out_shape=outs, in_specs=[pl.BlockSpec(memory_spac...  6.32 us
    ppermute x8, waiting for transfers between devices, swap(): return lax.ppermute(value, ('gx', 'gy', 'var'), pairs)  6.31 us
  transfers between devices with their start and end apart: 8, of which 6 were waited for; matrix products, arithmetic and copies ran while one was open for 0% of the time, Pallas kernels for 16%

profile of v2, /device:TPU:0, one launch (start us, length us, event | category | flops | bytes accessed | tf_op | source)
XLA Modules:
  0.0 21.9 jit_solution(14039919630832136820)
XLA Ops:
  0.0 1.6 %shard_map.91 = (f32[32,64,128]{2,1,0:T(8,128)S(1)}, f32[40,640]{1,0:T(8,128)S(1)}, bf16[80,128]{1,0:T(8,128)(2,1)S(1)}, bf16[128,256]{1,0:T(8,128)(2,1)S(1)}) custom-call(f32[1,32,64,128]{3,2,1,0:T(8,128)} %field_ref.1, bf16[4,80,128]{2,1,0:T(8,128)(2,1)} %constant.8.clone.tx_ref, bf16[2,128,256]{2,1,0:T(8,128)(2,1)} %constant.9.clone.ty_ref), custom_call_target="tpu_custom_call" | custom-call | tf_op jit(solution)/shard_map/pallas_call | solution.py:250
  1.6 0.6 %collective-permute-start = (f32[40,640]{1,0:T(8,128)S(1)}, f32[40,640]{1,0:T(8,128)S(1)}, u32[]{:S(2)}, u32[]{:S(2)}) collective-permute-start(f32[40,640]{1,0:T(8,128)S(1)} %get-tuple-element.19), channel_id=1, source_target_pairs={{0,8},{1,9},{2,10},{3,11},{4,12},{5,13},{6,14},{7,15},{8,0},{9,1},... | collective-permute-start | bytes 307208 | tf_op jit(solution)/shard_map/ppermute | solution.py:273
  2.2 0.5 %shard_map.92 = f32[40,640]{1,0:T(8,128)S(1)} custom-call(f32[32,64,128]{2,1,0:T(8,128)S(1)} %get-tuple-element.16.block_ref, bf16[80,128]{1,0:T(8,128)(2,1)S(1)} %get-tuple-element.17.tx_ref, bf16[128,256]{1,0:T(8,128)(2,1)S(1)} %get-tuple-element.18.ty_ref), custom_call_target="tpu_custom_call" | custom-call | flops 1000000000 | tf_op jit(solution)/shard_map/pallas_call | solution.py:250
  2.7 0.5 %collective-permute-done = f32[40,640]{1,0:T(8,128)S(1)} collective-permute-done((f32[40,640]{1,0:T(8,128)S(1)}, f32[40,640]{1,0:T(8,128)S(1)}, u32[]{:S(2)}, u32[]{:S(2)}) %collective-permute-start) | collective-permute-done | bytes 102432 | tf_op jit(solution)/shard_map/ppermute | solution.py:273
  3.2 3.9 %collective-permute-start.3 = (f32[40,640]{1,0:T(8,128)S(1)}, f32[40,640]{1,0:T(8,128)S(1)}, u32[]{:S(2)}, u32[]{:S(2)}) collective-permute-start(f32[40,640]{1,0:T(8,128)S(1)} %add.9._.own_ref), channel_id=1, source_target_pairs={{0,20},{1,21},{2,22},{3,23},{4,16},{5,17},{6,18},{7,19},{8,28},{9,... | collective-permute-start | bytes 307208 | tf_op jit(solution)/shard_map/ppermute | solution.py:273
  7.0 0.0 collective-permute-start.2
  7.0 0.3 %collective-permute-start.1 = (f32[40,640]{1,0:T(8,128)S(1)}, f32[40,640]{1,0:T(8,128)S(1)}, u32[]{:S(2)}, u32[]{:S(2)}) collective-permute-start(f32[40,640]{1,0:T(8,128)S(1)} %add.9._.own_ref), channel_id=1, source_target_pairs={{0,24},{1,25},{2,26},{3,27},{4,28},{5,29},{6,30},{7,31},{8,16},{9,... | collective-permute-start | bytes 307208 | tf_op jit(solution)/shard_map/ppermute | solution.py:273
  7.4 1.9 %shard_map.93 = (f32[40,640]{1,0:T(8,128)S(1)}, f32[40,640]{1,0:T(8,128)S(1)}, f32[32,128]{1,0:T(8,128)S(1)}, bf16[128,80]{1,0:T(8,128)(2,1)S(1)}, bf16[256,256]{1,0:T(8,128)(2,1)S(1)}) custom-call(f32[40,640]{1,0:T(8,128)S(1)} %add.9._.own_ref, s32[32]{0:T(128)} %keep_count_ref.1, s32[32]{0:T(128)} %class_ref.1, f32[8]{0:T(128)} %height_ref.1, ...), custom_call_target="tpu_custom_call" | custom-call | flops 1000000000 | tf_op jit(solution)/shard_map/pallas_call | solution.py:250
  9.3 1.2 %collective-permute-done.3.rest_2_ = f32[40,640]{1,0:T(8,128)S(1)} collective-permute-done((f32[40,640]{1,0:T(8,128)S(1)}, f32[40,640]{1,0:T(8,128)S(1)}, u32[]{:S(2)}, u32[]{:S(2)}) %collective-permute-start.3) | collective-permute-done | bytes 102432 | tf_op jit(solution)/shard_map/ppermute | solution.py:273
  10.5 1.7 %collective-permute-done.2.rest_1_ = f32[40,640]{1,0:T(8,128)S(1)} collective-permute-done((f32[40,640]{1,0:T(8,128)S(1)}, f32[40,640]{1,0:T(8,128)S(1)}, u32[]{:S(2)}, u32[]{:S(2)}) %collective-permute-start.2) | collective-permute-done | bytes 102432 | tf_op jit(solution)/shard_map/ppermute | solution.py:273
  12.2 0.0 collective-permute-done.1.rest_0_
  12.2 0.1 shard_map.94
  12.3 0.3 %collective-permute-start.7 = (f32[40,640]{1,0:T(8,128)S(1)}, f32[40,640]{1,0:T(8,128)S(1)}, u32[]{:S(2)}, u32[]{:S(2)}) collective-permute-start(f32[40,640]{1,0:T(8,128)S(1)} %get-tuple-element.23.delta_ref), channel_id=1, source_target_pairs={{0,8},{1,9},{2,10},{3,11},{4,12},{5,13},{6,14},{7,15},{8,0},{9,1},... | collective-permute-start | bytes 307208 | tf_op jit(solution)/shard_map/ppermute | solution.py:273
  12.6 0.2 %collective-permute-start.4 = (f32[8,128]{1,0:T(8,128)S(1)}, f32[8,128]{1,0:T(8,128)S(1)}, u32[]{:S(2)}, u32[]{:S(2)}) collective-permute-start(f32[8,128]{1,0:T(8,128)S(1)} %get-tuple-element.22), channel_id=1, source_target_pairs={{0,8},{1,9},{2,10},{3,11},{4,12},{5,13},{6,14},{7,15},{8,0},{9,1},... | collective-permute-start | bytes 12296 | tf_op jit(solution)/shard_map/ppermute | solution.py:273
  12.9 0.9 %collective-permute-done.4 = f32[8,128]{1,0:T(8,128)S(1)} collective-permute-done((f32[8,128]{1,0:T(8,128)S(1)}, f32[8,128]{1,0:T(8,128)S(1)}, u32[]{:S(2)}, u32[]{:S(2)}) %collective-permute-start.4) | collective-permute-done | bytes 4128 | tf_op jit(solution)/shard_map/ppermute | solution.py:273
  13.8 1.4 %collective-permute-start.5 = (f32[8,128]{1,0:T(8,128)S(1)}, f32[8,128]{1,0:T(8,128)S(1)}, u32[]{:S(2)}, u32[]{:S(2)}) collective-permute-start(f32[8,128]{1,0:T(8,128)S(1)} %add.10), channel_id=1, source_target_pairs={{0,9},{1,8},{2,11},{3,10},{4,13},{5,12},{6,15},{7,14},{8,1},{9,0},... | collective-permute-start | bytes 12296 | tf_op jit(solution)/shard_map/ppermute | solution.py:273
  15.2 0.6 %shard_map.95.own_ref = f32[16,64,128]{2,1,0:T(8,128)S(1)} custom-call(f32[40,640]{1,0:T(8,128)S(1)} %get-tuple-element.23.delta_ref, f32[32,128]{1,0:T(8,128)S(1)} %get-tuple-element.24.lift_ref, bf16[128,80]{1,0:T(8,128)(2,1)S(1)} %get-tuple-element.25.tx_ref, bf16[256,256]{1,0:T(8,128)(2,1)S(1)} %get-tuple-element.26.ty_ref), custom_call_target="tpu_custom_call" | custom-call | flops 1000000000 | tf_op jit(solution)/shard_map/pallas_call | solution.py:250
  15.8 1.0 %collective-permute-done.5 = f32[8,128]{1,0:T(8,128)S(1)} collective-permute-done((f32[8,128]{1,0:T(8,128)S(1)}, f32[8,128]{1,0:T(8,128)S(1)}, u32[]{:S(2)}, u32[]{:S(2)}) %collective-permute-start.5) | collective-permute-done | bytes 4128 | tf_op jit(solution)/shard_map/ppermute | solution.py:273
  16.8 2.4 %collective-permute-start.6 = (f32[8,128]{1,0:T(8,128)S(1)}, f32[8,128]{1,0:T(8,128)S(1)}, u32[]{:S(2)}, u32[]{:S(2)}) collective-permute-start(f32[8,128]{1,0:T(8,128)S(1)} %add.11.energy_ref), channel_id=1, source_target_pairs={{0,10},{1,11},{2,8},{3,9},{4,14},{5,15},{6,12},{7,13},{8,2},{9,3},... | collective-permute-start | bytes 12296 | tf_op jit(solution)/shard_map/ppermute | solution.py:273
  19.3 0.0 collective-permute-done.7.delta_ref
  19.3 0.6 %shard_map.96.other_ref = f32[16,64,128]{2,1,0:T(8,128)S(1)} custom-call(f32[40,640]{1,0:T(8,128)S(1)} %collective-permute-done.7.delta_ref, f32[32,128]{1,0:T(8,128)S(1)} %get-tuple-element.24.lift_ref, bf16[128,80]{1,0:T(8,128)(2,1)S(1)} %get-tuple-element.25.tx_ref, bf16[256,256]{1,0:T(8,128)(2,1)S(1)} %get-tuple-element.26.ty_ref), custom_call_target="tpu_custom_call" | custom-call | flops 1000000000 | tf_op jit(solution)/shard_map/pallas_call | solution.py:250
  19.9 0.9 %collective-permute-done.6.last_ref = f32[8,128]{1,0:T(8,128)S(1)} collective-permute-done((f32[8,128]{1,0:T(8,128)S(1)}, f32[8,128]{1,0:T(8,128)S(1)}, u32[]{:S(2)}, u32[]{:S(2)}) %collective-permute-start.6) | collective-permute-done | bytes 4128 | tf_op jit(solution)/shard_map/ppermute | solution.py:273
  20.8 1.1 %shard_map.97 = f32[1,32,64,128]{3,2,1,0:T(8,128)} custom-call(f32[8,128]{1,0:T(8,128)S(1)} %add.11.energy_ref, f32[8,128]{1,0:T(8,128)S(1)} %collective-permute-done.6.last_ref, f32[32,64,128]{2,1,0:T(8,128)S(1)} %get-tuple-element.16.block_ref, f32[16,64,128]{2,1,0:T(8,128)S(1)} %shard_map.95.own_ref, f32[16,64,128]{2,1,0:T(8,128)S(1)} %shard_map.96.other_ref), custom_call_target="tpu_custom_call" | custom-call | tf_op jit(solution)/shard_map/pallas_call | solution.py:250
  (3 shorter events, 0.0 us)
Async XLA Ops:
  1.6 1.5 %collective-permute-start = (f32[40,640]{1,0:T(8,128)S(1)}, f32[40,640]{1,0:T(8,128)S(1)}, u32[]{:S(2)}, u32[]{:S(2)}) collective-permute-start(f32[40,640]{1,0:T(8,128)S(1)} %get-tuple-element.19), channel_id=1, source_target_pairs={{0,8},{1,9},{2,10},{3,11},{4,12},{5,13},{6,14},{7,15},{8,0},{9,1},... | collective-permute-start | bytes 307208 | tf_op jit(solution)/shard_map/ppermute | solution.py:273
  3.2 7.3 %collective-permute-start.3 = (f32[40,640]{1,0:T(8,128)S(1)}, f32[40,640]{1,0:T(8,128)S(1)}, u32[]{:S(2)}, u32[]{:S(2)}) collective-permute-start(f32[40,640]{1,0:T(8,128)S(1)} %add.9._.own_ref), channel_id=1, source_target_pairs={{0,20},{1,21},{2,22},{3,23},{4,16},{5,17},{6,18},{7,19},{8,28},{9,... | collective-permute-start | bytes 307208 | tf_op jit(solution)/shard_map/ppermute | solution.py:273
  7.0 5.2 %collective-permute-start.2 = (f32[40,640]{1,0:T(8,128)S(1)}, f32[40,640]{1,0:T(8,128)S(1)}, u32[]{:S(2)}, u32[]{:S(2)}) collective-permute-start(f32[40,640]{1,0:T(8,128)S(1)} %add.9._.own_ref), channel_id=1, source_target_pairs={{0,12},{1,13},{2,14},{3,15},{4,8},{5,9},{6,10},{7,11},{8,4},{9,5},... | collective-permute-start | bytes 307208 | tf_op jit(solution)/shard_map/ppermute | solution.py:273
  7.0 5.2 %collective-permute-start.1 = (f32[40,640]{1,0:T(8,128)S(1)}, f32[40,640]{1,0:T(8,128)S(1)}, u32[]{:S(2)}, u32[]{:S(2)}) collective-permute-start(f32[40,640]{1,0:T(8,128)S(1)} %add.9._.own_ref), channel_id=1, source_target_pairs={{0,24},{1,25},{2,26},{3,27},{4,28},{5,29},{6,30},{7,31},{8,16},{9,... | collective-permute-start | bytes 307208 | tf_op jit(solution)/shard_map/ppermute | solution.py:273
  12.3 7.0 %collective-permute-start.7 = (f32[40,640]{1,0:T(8,128)S(1)}, f32[40,640]{1,0:T(8,128)S(1)}, u32[]{:S(2)}, u32[]{:S(2)}) collective-permute-start(f32[40,640]{1,0:T(8,128)S(1)} %get-tuple-element.23.delta_ref), channel_id=1, source_target_pairs={{0,8},{1,9},{2,10},{3,11},{4,12},{5,13},{6,14},{7,15},{8,0},{9,1},... | collective-permute-start | bytes 307208 | tf_op jit(solution)/shard_map/ppermute | solution.py:273
  12.6 1.2 %collective-permute-start.4 = (f32[8,128]{1,0:T(8,128)S(1)}, f32[8,128]{1,0:T(8,128)S(1)}, u32[]{:S(2)}, u32[]{:S(2)}) collective-permute-start(f32[8,128]{1,0:T(8,128)S(1)} %get-tuple-element.22), channel_id=1, source_target_pairs={{0,8},{1,9},{2,10},{3,11},{4,12},{5,13},{6,14},{7,15},{8,0},{9,1},... | collective-permute-start | bytes 12296 | tf_op jit(solution)/shard_map/ppermute | solution.py:273
  13.8 3.0 %collective-permute-start.5 = (f32[8,128]{1,0:T(8,128)S(1)}, f32[8,128]{1,0:T(8,128)S(1)}, u32[]{:S(2)}, u32[]{:S(2)}) collective-permute-start(f32[8,128]{1,0:T(8,128)S(1)} %add.10), channel_id=1, source_target_pairs={{0,9},{1,8},{2,11},{3,10},{4,13},{5,12},{6,15},{7,14},{8,1},{9,0},... | collective-permute-start | bytes 12296 | tf_op jit(solution)/shard_map/ppermute | solution.py:273
  16.8 3.9 %collective-permute-start.6 = (f32[8,128]{1,0:T(8,128)S(1)}, f32[8,128]{1,0:T(8,128)S(1)}, u32[]{:S(2)}, u32[]{:S(2)}) collective-permute-start(f32[8,128]{1,0:T(8,128)S(1)} %add.11.energy_ref), channel_id=1, source_target_pairs={{0,10},{1,11},{2,8},{3,9},{4,14},{5,15},{6,12},{7,13},{8,2},{9,3},... | collective-permute-start | bytes 12296 | tf_op jit(solution)/shard_map/ppermute | solution.py:273
